TPU v7x, 128 devices: a whole 4x4x4 slice. The times are simulated.
128 devices in a mesh: gx: 16 (over y, x), gy: 8 (over z, core).
Axes of the slice: x: 4, y: 4, z: 4, core: 2. Of those that a mesh axis runs over, the one named last changes fastest.
Arguments:
- point_feats: bfloat16 [1048576, 128], P(('gx', 'gy')), may hold values from -6 to 6
- point_tile: int32 [1048576, 1], P(('gx', 'gy')), may hold values from 0 to 127; in each aligned block of 8192 rows (0 to 8191, 8192 to 16383, ...) at most 80 rows name the same one
- point_cell: int32 [1048576], P(('gx', 'gy')), may hold values from 0 to 4095
- point_count: int32 [128], P(('gx', 'gy')), may hold values from 6144 to 8192, as said below
- conv_weight: bfloat16 [3, 3, 128, 128], replicated, may hold values from -0.1875 to 0.1875
- conv_bias: float32 [128], replicated, may hold values from -3 to 3
Outputs:
- bev_map: bfloat16 [256, 2048, 128], P('gx', 'gy')
- conv_out: bfloat16 [256, 2048, 128], P('gx', 'gy')
Inputs may be any that keep to these rules, and one draw needn't show every extreme that they name: `point_tile`: among the 8192 rows of one device no tile is named by more than 80 rows, a bound that some block reaches. `point_count`: only slots below a device's count are live; some device has all 8192 slots live.
All inputs are finite; a program needn't handle non-finite values.
Results may differ from a plain program's by a relative error of at most 0.0045.
Values may be sent and summed in bfloat16 or wider, within the bound.
A program may use at most 64 MiB of HBM per device.

v0:
```python
import jax
import jax.numpy as jnp
from jax import lax
from jax.sharding import PartitionSpec as P

COLS_DEV = 256
ROWS_DEV = 16


def with_halo(cells, sides, width):
    for axis, dim in sides:
        count = lax.axis_size(axis)
        ends = count - 1
        head = lax.slice_in_dim(cells, 0, width, axis=dim)
        tail = lax.slice_in_dim(cells, cells.shape[dim] - width, cells.shape[dim], axis=dim)
        cells = jnp.concatenate(
            [
                lax.ppermute(tail, axis, [(i, (i + 1) % count) for i in range(ends)]),
                cells,
                lax.ppermute(head, axis, [((i + 1) % count, i) for i in range(ends)]),
            ],
            axis=dim,
        )
    return cells


def shards(point_feats, point_tile, point_cell, point_count, conv_weight, conv_bias):
    size_gx = lax.axis_size("gx")
    size_gy = lax.axis_size("gy")
    devices = size_gx * size_gy
    points = point_feats.shape[0]
    channels = point_feats.shape[1]
    capacity = 5 * points // (4 * devices)
    slots = devices * capacity
    target = point_tile[:, 0]
    live = jnp.arange(points, dtype=jnp.int32) < point_count[0]
    hits = (target[:, None] == jnp.arange(devices, dtype=jnp.int32)[None, :]) & live[:, None]
    blk = min(128, points)
    nblk = points // blk
    inner_idx = jnp.arange(blk, dtype=jnp.int32)
    lower = (inner_idx[:, None] >= inner_idx[None, :]).astype(jnp.bfloat16)
    hit_blocks = hits.astype(jnp.bfloat16).reshape(nblk, blk, devices)
    inner = jnp.einsum("ij,bjd->bid", lower, hit_blocks, preferred_element_type=jnp.float32)
    totals = inner[:, -1, :]
    before = jnp.cumsum(totals, axis=0) - totals
    ranks = (inner + before[:, None, :]).reshape(points, devices)
    place = jnp.sum(jnp.where(hits, ranks, 0.0), axis=1).astype(jnp.int32) - 1
    position = jnp.where(live, target * capacity + place, slots)
    slot_ids = jnp.arange(slots, dtype=jnp.int32)

    def pick(found, item):
        pos_block, first = item
        matches = pos_block[:, None] == slot_ids[None, :]
        owners = (first + inner_idx + 1)[:, None]
        return (found + jnp.sum(jnp.where(matches, owners, 0), axis=0), None)

    starts = jnp.arange(nblk, dtype=jnp.int32) * blk
    source, unused = lax.scan(
        pick, jnp.zeros((slots,), jnp.int32), (position.reshape(nblk, blk), starts)
    )
    filled = source > 0
    source_row = jnp.maximum(source - 1, 0)
    send_feats = jnp.where(
        filled[:, None], jnp.take(point_feats, source_row, axis=0), jnp.zeros((), jnp.bfloat16)
    )
    send_cells = jnp.where(filled, jnp.take(point_cell, source_row, axis=0), -1)
    got_feats, got_cells = (
        lax.all_to_all(
            send_feats.reshape(devices, capacity, channels),
            ("gx", "gy"),
            split_axis=0,
            concat_axis=0,
            tiled=True,
        ),
        lax.all_to_all(
            send_cells.reshape(devices, capacity),
            ("gx", "gy"),
            split_axis=0,
            concat_axis=0,
            tiled=True,
        ),
    )
    got_feats = got_feats.reshape(-1, channels)
    got_cells = got_cells.reshape(-1)
    col_ids = jnp.arange(COLS_DEV, dtype=jnp.int32)

    def one_row(row):
        wanted = row * COLS_DEV + col_ids
        onehot = (wanted[:, None] == got_cells[None, :]).astype(jnp.bfloat16)
        return jnp.dot(onehot, got_feats, preferred_element_type=jnp.float32)

    sums = lax.map(one_row, jnp.arange(ROWS_DEV, dtype=jnp.int32))
    bev_map = sums.astype(jnp.bfloat16)
    padded = with_halo(bev_map, (("gx", 0), ("gy", 1)), 1)
    total = jnp.zeros((ROWS_DEV, COLS_DEV, channels), jnp.float32)
    for shift_row in range(3):
        for shift_col in range(3):
            window = padded[shift_row : shift_row + ROWS_DEV, shift_col : shift_col + COLS_DEV]
            total = total + jnp.einsum(
                "rcd,de->rce",
                window,
                conv_weight[shift_row, shift_col],
                preferred_element_type=jnp.float32,
            )
    conv_out = jax.nn.relu(total + conv_bias).astype(jnp.bfloat16)
    return (bev_map, conv_out)


def solution(mesh):
    in_specs = (
        P(("gx", "gy"), None),
        P(("gx", "gy"), None),
        P(("gx", "gy")),
        P(("gx", "gy")),
        P(),
        P(),
    )
    out_specs = (P("gx", "gy", None), P("gx", "gy", None))
    return jax.shard_map(shards, mesh=mesh, in_specs=in_specs, out_specs=out_specs, check_vma=False)
```

profile of v0, /device:TPU:7, one launch (start us, length us, event | category | flops | bytes accessed | tf_op | source)
XLA Modules:
  0.0 402.9 jit_solution(16874526411669957181)
XLA Ops:
  1.5 10.3 %fusion.20 = f32[64,128,128]{2,1,0:T(8,128)S(1)} fusion(s32[64,128]{1,0:T(8,128)} %bitcast.88, pred[64,128]{1,0:T(8,128)(4,1)S(1)} %add_compare_fusion), kind=kOutput, calls=%fused_computation.23 | convolution fusion | flops 270548992 | bytes 4235264 | tf_op jit(solution)/shard_map/ij,bjd->bid/dot_general | solution.py:43
  11.9 4.1 %select_reduce_fusion.1 = f32[64,128]{1,0:T(8,128)S(1)} fusion(f32[64,128,128]{2,1,0:T(8,128)S(1)} %fusion.20, f32[64,128]{1,0:T(8,128)S(1)} %bitcast.92, s32[64,128]{1,0:T(8,128)S(1)} %bitcast.89, pred[64,128]{1,0:T(8,128)(4,1)S(1)} %add_compare_fusion), kind=kLoop, calls=%fused_computation.18 | loop fusion | flops 5234688 | bytes 4300800 | tf_op jit(solution)/shard_map/reduce_sum | solution.py:47
  16.1 134.9 %while.25 = (s32[]{:T(128)}, s32[10240]{0:T(1024)S(1)}, s32[64,128]{1,0:T(8,128)S(1)}, s32[64]{0:T(128)S(1)}) while((s32[]{:T(128)}, s32[10240]{0:T(1024)S(1)}, s32[64,128]{1,0:T(8,128)S(1)}, s32[64]{0:T(128)S(1)}) %tuple.57), condition=%wide.region_4.5_spmd.clone.clone, body=%wide.region_2.4_spmd.clone.sunk.clone | while | flops 3942659 | bytes 166483 | solution.py:58
  21.6 0.8 select_reduce_fusion.4
  23.7 0.8 select_reduce_fusion.4
  30.0 0.8 select_reduce_fusion.4
  32.1 0.8 select_reduce_fusion.4
  36.3 0.8 select_reduce_fusion.4
  38.4 0.8 select_reduce_fusion.4
  40.6 0.8 select_reduce_fusion.4
  44.8 0.8 select_reduce_fusion.4
  46.9 0.8 select_reduce_fusion.4
  53.2 0.8 select_reduce_fusion.4
  55.3 0.8 select_reduce_fusion.4
  61.6 0.8 select_reduce_fusion.4
  63.7 0.8 select_reduce_fusion.4
  70.1 0.8 select_reduce_fusion.4
  72.2 0.8 select_reduce_fusion.4
  76.4 0.8 select_reduce_fusion.4
  78.5 0.8 select_reduce_fusion.4
  80.6 0.8 select_reduce_fusion.4
  84.8 0.8 select_reduce_fusion.4
  86.9 0.8 select_reduce_fusion.4
  93.2 0.8 select_reduce_fusion.4
  95.4 0.8 select_reduce_fusion.4
  101.7 0.8 select_reduce_fusion.4
  103.8 0.8 select_reduce_fusion.4
  110.1 0.8 select_reduce_fusion.4
  112.2 0.8 select_reduce_fusion.4
  116.4 0.8 select_reduce_fusion.4
  118.5 0.8 select_reduce_fusion.4
  120.7 0.8 select_reduce_fusion.4
  124.9 0.8 select_reduce_fusion.4
  127.0 0.8 select_reduce_fusion.4
  151.0 56.8 %gather_fusion = s32[10240]{0:T(1024)S(1)} fusion(s32[8192]{0:T(1024)S(1)} %copy-done.1, s32[10240]{0:T(1024)S(1)} %fusion.49), kind=kCustom, calls=%fused_computation | custom fusion | bytes 122880 | tf_op jit(solution)/shard_map/jit(_take)/gather | solution.py:66
  208.5 10.8 %all-to-all-start = ((s32[128,1,80]{2,1,0:T(1,128)}), s32[128,1,80]{2,1,0:T(1,128)S(1)}, u32[]{:S(2)}, u32[]{:S(2)}) async-start(s32[128,1,80]{2,1,0:T(1,128)} %bitcast.5), calls=%async_computation | async-start | bytes 131072 | tf_op jit(solution)/shard_map/all_to_all | solution.py:75
  219.5 36.1 %gather_fusion.1 = bf16[10240,128]{1,0:T(8,128)(2,1)} fusion(bf16[8192,128]{1,0:T(8,128)(2,1)S(1)} %copy-done, s32[10240]{0:T(1024)S(1)} %fusion.49), kind=kCustom, calls=%fused_computation.1 | custom fusion | bytes 5283840 | tf_op jit(solution)/shard_map/jit(_take)/gather | solution.py:64
  255.6 5.7 %select_select_fusion = bf16[128,80,128]{2,1,0:T(8,128)(2,1)} fusion(bf16[128,80,128]{2,1,0:T(8,128)(2,1)} %bitcast.87, pred[128,80]{1,0:T(8,128)(4,1)S(1)} %broadcast_in_dim.81, pred[128,80]{1,0:T(8,128)(4,1)S(1)} %broadcast_in_dim.79), kind=kLoop, calls=%fused_computation.22 | loop fusion | flops 2621440 | bytes 5263360 | tf_op jit(solution)/shard_map/jit(_where)/select_n | solution.py:63
  261.4 10.2 %all-to-all-start.1 = ((bf16[128,80,128]{2,1,0:T(8,128)(2,1)}), bf16[128,80,128]{2,1,0:T(8,128)(2,1)}, u32[]{:S(2)}, u32[]{:S(2)}) async-start(bf16[128,80,128]{2,1,0:T(8,128)(2,1)} %select_select_fusion), calls=%async_computation.1 | async-start | bytes 5242880 | tf_op jit(solution)/shard_map/all_to_all | solution.py:68
  271.7 33.7 %all-to-all-done.1 = bf16[128,80,128]{2,1,0:T(8,128)(2,1)} async-done(((bf16[128,80,128]{2,1,0:T(8,128)(2,1)}), bf16[128,80,128]{2,1,0:T(8,128)(2,1)}, u32[]{:S(2)}, u32[]{:S(2)}) %all-to-all-start.1) | async-done | bytes 2621472 | tf_op jit(solution)/shard_map/all_to_all | solution.py:68
  305.4 73.6 %while.26 = (s32[]{:T(128)}, bf16[16,256,128]{2,1,0:T(8,128)(2,1)S(1)}, s32[16]{0:T(128)S(1)}, bf16[10240,128]{1,0:T(8,128)(2,1)}, s32[10240]{0:T(1024)S(1)}, /*index=5*/s32[1]{0:T(128)}) while((s32[]{:T(128)}, bf16[16,256,128]{2,1,0:T(8,128)(2,1)S(1)}, s32[16]{0:T(128)S(1)}, bf16[10240,128]{1,0:T(8,128)(2,1)}, ...), condition=%wide.wide.region_6.7_spmd.clone.clone, body=%wide.wide.region_5.6_spmd.clone.sunk.clone | while | flops 673710336 | bytes 2795621 | solution.py:92
  306.6 3.3 fusion.91
  311.2 3.3 fusion.91
  315.8 3.3 fusion.91
  320.4 3.3 fusion.91
  325.0 3.3 fusion.91
  329.6 3.3 fusion.91
  334.2 3.3 fusion.91
  338.8 3.3 fusion.91
  343.4 3.3 fusion.91
  348.0 3.3 fusion.91
  352.6 3.3 fusion.91
  357.2 3.3 fusion.91
  361.8 3.3 fusion.91
  366.4 3.3 fusion.91
  371.0 3.3 fusion.91
  375.6 3.3 fusion.91
  379.0 3.6 collective-permute-start
  382.6 1.9 collective-permute-start.1
  385.0 4.8 %collective-permute-done.1 = bf16[1,256,128]{2,1,0:T(8,128)(2,1)S(1)} collective-permute-done((bf16[1,256,128]{2,1,0:T(8,128)(2,1)S(1)}, bf16[1,256,128]{2,1,0:T(8,128)(2,1)S(1)}, u32[]{:S(2)}, u32[]{:S(2)}) %collective-permute-start.1) | collective-permute-done | bytes 65568 | tf_op jit(solution)/shard_map/ppermute | solution.py:20
  389.8 3.1 collective-permute-start.2
  392.9 3.0 collective-permute-start.3
  396.7 1.1 collective-permute-done.3
  400.9 2.1 maximum_convert_fusion
  (360 shorter events, 123.0 us)
Async XLA Ops:
  0.6 218.9 %copy-start = (bf16[8192,128]{1,0:T(8,128)(2,1)S(1)}, bf16[8192,128]{1,0:T(8,128)(2,1)}, u32[]{:S(2)}) copy-start(bf16[8192,128]{1,0:T(8,128)(2,1)} %param.10) | copy-start | bytes 6291460
  1.5 10.4 %copy-start.4 = (s32[8192,1]{0,1:T(1,128)S(1)}, s32[8192,1]{0,1:T(1,128)}, u32[]{:S(2)}) copy-start(s32[8192,1]{0,1:T(1,128)} %param.11) | copy-start | bytes 98308
  11.9 139.1 %copy-start.1 = (s32[8192]{0:T(1024)S(1)}, s32[8192]{0:T(1024)}, u32[]{:S(2)}) copy-start(s32[8192]{0:T(1024)} %param.12) | copy-start | bytes 98308
  208.5 52.8 %all-to-all-start = ((s32[128,1,80]{2,1,0:T(1,128)}), s32[128,1,80]{2,1,0:T(1,128)S(1)}, u32[]{:S(2)}, u32[]{:S(2)}) async-start(s32[128,1,80]{2,1,0:T(1,128)} %bitcast.5), calls=%async_computation | async-start | bytes 131072 | tf_op jit(solution)/shard_map/all_to_all | solution.py:75
  261.4 44.0 %all-to-all-start.1 = ((bf16[128,80,128]{2,1,0:T(8,128)(2,1)}), bf16[128,80,128]{2,1,0:T(8,128)(2,1)}, u32[]{:S(2)}, u32[]{:S(2)}) async-start(bf16[128,80,128]{2,1,0:T(8,128)(2,1)} %select_select_fusion), calls=%async_computation.1 | async-start | bytes 5242880 | tf_op jit(solution)/shard_map/all_to_all | solution.py:68
  305.4 79.2 %copy-start.3 = (bf16[3,3,128,128]{3,2,1,0:T(8,128)(2,1)S(1)}, bf16[3,3,128,128]{3,2,1,0:T(8,128)(2,1)}, u32[]{:S(2)}) copy-start(bf16[3,3,128,128]{3,2,1,0:T(8,128)(2,1)} %param.14) | copy-start | bytes 884740
  379.0 18.8 %copy-start.2 = (bf16[16,256,128]{2,1,0:T(8,128)(2,1)}, bf16[16,256,128]{2,1,0:T(8,128)(2,1)S(1)}, u32[]{:S(2)}) copy-start(bf16[16,256,128]{2,1,0:T(8,128)(2,1)S(1)} %get-tuple-element.67) | copy-start | bytes 3145732
  379.0 6.0 %collective-permute-start = (bf16[1,256,128]{2,1,0:T(8,128)(2,1)S(1)}, bf16[1,256,128]{2,1,0:T(8,128)(2,1)S(1)}, u32[]{:S(2)}, u32[]{:S(2)}) collective-permute-start(bf16[1,256,128]{2,1,0:T(8,128)(2,1)S(1)} %get-tuple-element.124), channel_id=1, source_target_pairs={{0,8},{8,16},{16,24},{24,32},{32,40},{40,48},{48,56},{56,64},{64,7... | collective-permute-start | bytes 196616 | tf_op jit(solution)/shard_map/ppermute | solution.py:18
  382.6 7.1 %collective-permute-start.1 = (bf16[1,256,128]{2,1,0:T(8,128)(2,1)S(1)}, bf16[1,256,128]{2,1,0:T(8,128)(2,1)S(1)}, u32[]{:S(2)}, u32[]{:S(2)}) collective-permute-start(bf16[1,256,128]{2,1,0:T(8,128)(2,1)S(1)} %get-tuple-element.125), channel_id=1, source_target_pairs={{8,0},{16,8},{24,16},{32,24},{40,32},{48,40},{56,48},{64,56},{72,6... | collective-permute-start | bytes 196616 | tf_op jit(solution)/shard_map/ppermute | solution.py:20
  389.8 7.0 %collective-permute-start.2 = (bf16[18,1,128]{2,1,0:T(2,128)(2,1)S(1)}, bf16[18,1,128]{2,1,0:T(2,128)(2,1)S(1)}, u32[]{:S(2)}, u32[]{:S(2)}) collective-permute-start(bf16[18,1,128]{2,1,0:T(2,128)(2,1)S(1)} %get-tuple-element.123), channel_id=1, source_target_pairs={{0,1},{1,2},{2,3},{3,4},{4,5},{5,6},{6,7},{8,9},{9,10},{10,11},{11... | collective-permute-start | bytes 13832 | tf_op jit(solution)/shard_map/ppermute | solution.py:18
  392.9 5.0 %collective-permute-start.3 = (bf16[18,1,128]{2,1,0:T(2,128)(2,1)S(1)}, bf16[18,1,128]{2,1,0:T(2,128)(2,1)S(1)}, u32[]{:S(2)}, u32[]{:S(2)}) collective-permute-start(bf16[18,1,128]{2,1,0:T(2,128)(2,1)S(1)} %get-tuple-element.122), channel_id=1, source_target_pairs={{1,0},{2,1},{3,2},{4,3},{5,4},{6,5},{7,6},{9,8},{10,9},{11,10},{12... | collective-permute-start | bytes 13832 | tf_op jit(solution)/shard_map/ppermute | solution.py:20
  400.2 0.7 copy-start.5
where the time goes:
time: 405 us; the launch traced here: 403 us
  local copies, waits for them, and re-layouts  146 us (36%)
  other arithmetic  100 us (25%)
  matrix products  69.2 us (17%)
  waiting for transfers between devices  39.6 us (10%)
  starting transfers between devices  32.5 us (8%)
  loops' own time  13.9 us (3%)
    gather x1, local copies, waits for them, and re-layouts, shards(): send_cells = jnp.where(filled, jnp.take(point_cell, source_row, axis=0), -1)  56.8 us
    dot_general x16, matrix products, one_row(): return jnp.dot(onehot, got_feats, preferred_element_type=jnp.float32)  53.4 us
    reduce_sum x64, other arithmetic, pick(): return (found + jnp.sum(jnp.where(matches, owners, 0), axis=0), None)  48.8 us
    dynamic_slice x64, local copies, waits for them, and re-layouts, shards(): lax.scan(pick, jnp.zeros((slots,), jnp.int32), (position.reshape(nblk, bl...  41.6 us
    add x64, other arithmetic, pick(): owners = (first + inner_idx + 1)[:, None]  39.9 us
    gather x1, local copies, waits for them, and re-layouts, shards(): jnp.take(point_feats, source_row, axis=0)  36.1 us
    all_to_all x1, waiting for transfers between devices, shards(): lax.all_to_all(send_feats.reshape(devices, capacity, channels), ('gx', 'g...  33.7 us
    another operation x1, loops' own time, shards(): sums = lax.map(one_row, jnp.arange(ROWS_DEV, dtype=jnp.int32))  10.8 us
  transfers between devices with their start and end apart: 6, of which 3 were waited for; matrix products, arithmetic and copies ran while one was open for 11% of the time, Pallas kernels for 0%

commit v1 on v0

v1 whole, which is shorter than its diff:
```python
import functools

import jax
import jax.numpy as jnp
from jax import lax
from jax.experimental import pallas as pl
from jax.experimental.pallas import tpu as pltpu
from jax.sharding import PartitionSpec as P

MESH = pl.DeviceIdType.MESH
F32 = jnp.float32
BF16 = jnp.bfloat16
C = 128
COLS = 256
ROWS = 16
POINTS = 8192
CAP = 80
DEV = 128
GROUP = 16
GROUPS = DEV // GROUP
SPAN = GROUP * CAP
STRIDE = 45
BLOCK = 512


def iota(shape, dim):
    return lax.broadcasted_iota(jnp.int32, shape, dim)


def index_kernel(tile_ref, cell_ref, count_ref, inv_ref, send_cell_ref, offs, table):
    offs[...] = jnp.zeros_like(offs)
    table[...] = jnp.zeros_like(table)
    upper = (iota((BLOCK, BLOCK), 0) <= iota((BLOCK, BLOCK), 1)).astype(BF16)
    ones = jnp.ones((BLOCK, 128), BF16)
    count = count_ref[0]

    def step(b, carry):
        tile = tile_ref[pl.ds(b, 1), :]
        cell = cell_ref[pl.ds(b, 1), :]
        p = b * BLOCK + iota((1, BLOCK), 1)
        tile = jnp.where(p < count, tile, DEV)
        hit = iota((DEV, BLOCK), 0) == tile
        hit16 = hit.astype(F32).astype(BF16)
        cum = jnp.dot(hit16, upper, preferred_element_type=F32)
        base = jnp.concatenate([offs[...]] * (BLOCK // 128), axis=1)
        rank = jnp.sum(jnp.where(hit, cum + base, 0.0), axis=0, keepdims=True) - 1.0
        offs[...] += jnp.dot(hit16, ones, preferred_element_type=F32)
        slot = iota((128, BLOCK), 0).astype(F32) == rank
        parts = []
        for value in ((p >> 8) + 1, p & 255, cell >> 8, cell & 255):
            parts.append(jnp.where(slot, value.astype(F32), 0.0).astype(BF16))
        table[...] += lax.dot_general(
            hit16,
            jnp.concatenate(parts, axis=0),
            (((1,), (1,)), ((), ())),
            preferred_element_type=F32,
        )
        return carry

    lax.fori_loop(0, POINTS // BLOCK, step, 0)
    high = table[:, 0:128]
    filled = high > 0.0
    source = (high - 1.0) * 256.0 + table[:, 128:256]
    inv_ref[...] = jnp.where(filled, source, float(POINTS)).astype(jnp.int32)
    send_cell_ref[...] = jnp.where(filled, table[:, 256:384] * 256.0 + table[:, 384:512], -1.0)


def place():
    gx = lax.axis_index("gx")
    gy = lax.axis_index("gy")
    return lax.rem(gx, 4), lax.div(gx, 4), lax.div(gy, 2), lax.rem(gy, 2)


def partner(i):
    x, y, z, c = place()
    o = lax.rem(i * STRIDE, DEV)
    tc = lax.rem(c + lax.rem(o, 2), 2)
    tz = lax.rem(z + lax.rem(lax.div(o, 2), 4), 4)
    tx = lax.rem(x + lax.rem(lax.div(o, 8), 4), 4)
    ty = lax.rem(y + lax.div(o, 32), 4)
    return ty * 4 + tx, tz * 2 + tc


def main_kernel(
    inv_ref, feats_ref, cell_ref, w_ref, bias_ref, bev_ref, conv_ref,
    src, stage, send, recv, cells_in, acc, expand, onehot, row_bc, xs, wmat, bev, top, bottom,
    col_send, col_recv, corner_send, corner_recv, ext, edge, stage_col,
    send_sem, cell_send_sem, recv_sem, cell_sem, halo_send_sem, halo_sem,
):
    gx = lax.axis_index("gx")
    gy = lax.axis_index("gy")
    zero_row = jnp.zeros((COLS, C), BF16)
    top[...] = zero_row
    bottom[...] = zero_row
    col_recv[...] = jnp.zeros_like(col_recv)
    corner_recv[...] = jnp.zeros_like(corner_recv)

    barrier = pltpu.get_barrier_semaphore()

    def greet(i, carry):
        pl.semaphore_signal(barrier, inc=1, device_id=partner(i), device_id_type=MESH)
        return carry

    lax.fori_loop(1, DEV, greet, 0)

    def widen(b, carry):
        at = pl.multiple_of(b * 256, 256)
        src[pl.ds(at, 256), :] = feats_ref[pl.ds(at, 256), :].astype(F32)
        return carry

    lax.fori_loop(0, POINTS // 256, widen, 0)
    src[pl.ds(POINTS, 8), :] = jnp.zeros((8, C), F32)
    for a in range(3):
        for b in range(3):
            wmat[a * C : (a + 1) * C, b * C : (b + 1) * C] = w_ref[a, b]
    acc[...] = jnp.zeros_like(acc)
    lane = iota((1, SPAN), 1).astype(F32)
    owner = jnp.floor((lane + 0.5) * (1.0 / CAP))
    within = lane - owner * CAP
    expand[...] = (iota((128, SPAN), 0).astype(F32) == within).astype(F32).astype(BF16)

    pl.semaphore_wait(barrier, DEV - 1)

    def cell_copy(i, dest):
        return pltpu.make_async_remote_copy(
            src_ref=cell_ref.at[dest[0] * 8 + dest[1]],
            dst_ref=cells_in.at[i],
            send_sem=cell_send_sem,
            recv_sem=cell_sem.at[lax.div(i, GROUP)],
            device_id=dest,
            device_id_type=MESH,
        )

    def feat_copy(i):
        return pltpu.make_async_remote_copy(
            src_ref=send.at[i],
            dst_ref=recv.at[i],
            send_sem=send_sem,
            recv_sem=recv_sem.at[lax.div(i, GROUP)],
            device_id=partner(i),
            device_id_type=MESH,
        )

    def send_cells(i, carry):
        cell_copy(i, partner(i)).start()
        return carry

    lax.fori_loop(1, DEV, send_cells, 0)

    def pack(tile):
        for k in range(CAP):
            stage[k : k + 1, :] = src[pl.ds(inv_ref[tile, k], 1), :]
        return stage[...].astype(BF16)

    own = gx * 8 + gy
    recv[0] = pack(own)
    cells_in[0] = cell_ref[own]

    def pack_and_send(i, carry):
        dest = partner(i)
        send[i] = pack(dest[0] * 8 + dest[1])

        @pl.when(i > 1)
        def _():
            feat_copy(i - 1).start()

        return carry

    lax.fori_loop(1, DEV, pack_and_send, 0)
    feat_copy(DEV - 1).start()

    eye = iota((128, 128), 0) == iota((128, 128), 1)
    ones = jnp.ones((128, 128), BF16)
    mine = iota((GROUP, SPAN), 0).astype(F32) == owner

    def scatter(g):
        for j in range(GROUP):
            xs[j : j + 1, :] = cells_in[g * GROUP + j]
        cell = xs[...]
        row = jnp.floor(cell * (1.0 / COLS))
        col = cell - row * COLS
        both = jnp.concatenate([row, col], axis=0).astype(BF16)
        dense = jnp.dot(both, expand[...], preferred_element_type=F32)
        row_line = jnp.sum(jnp.where(mine, dense[0:GROUP], 0.0), axis=0, keepdims=True)
        col_line = jnp.sum(jnp.where(mine, dense[GROUP:], 0.0), axis=0, keepdims=True)
        onehot[...] = (iota((COLS, SPAN), 0).astype(F32) == col_line).astype(F32).astype(BF16)
        for q in range(SPAN // 128):
            span = slice(q * 128, (q + 1) * 128)
            diag = jnp.where(eye, row_line[:, span], 0.0).astype(BF16)
            row_bc[span, :] = jnp.dot(diag, ones, preferred_element_type=F32).astype(BF16)
        feats = recv[pl.ds(pl.multiple_of(g * GROUP, GROUP), GROUP)].reshape(SPAN, C)
        rows = row_bc[...]
        none = jnp.zeros((), BF16)
        for pair in range(ROWS // 2):
            even = jnp.where(rows == jnp.asarray(2 * pair, BF16), feats, none)
            odd = jnp.where(rows == jnp.asarray(2 * pair + 1, BF16), feats, none)
            acc[pair] += jnp.dot(
                onehot[...], jnp.concatenate([even, odd], axis=1), preferred_element_type=F32
            )

    def landed(g, first):
        at = pl.ds(g * GROUP + first, GROUP - first)
        pltpu.make_async_copy(cells_in.at[at], cells_in.at[at], cell_sem.at[g]).wait()
        pltpu.make_async_copy(recv.at[at], recv.at[at], recv_sem.at[g]).wait()

    landed(0, 1)
    scatter(0)

    def absorb(g, carry):
        landed(g, 0)
        scatter(g)
        return carry

    lax.fori_loop(1, GROUPS, absorb, 0)

    for r in range(ROWS):
        half = slice((r % 2) * C, (r % 2 + 1) * C)
        line = acc[r // 2, :, half]
        rounded = line.astype(BF16)
        bev[r] = rounded
        bev_ref[r] = rounded
        stage_col[0, r : r + 1, :] = line[0:1, :]
        stage_col[1, r : r + 1, :] = line[COLS - 1 : COLS, :]
    col_send[0] = stage_col[0].astype(BF16)
    col_send[1] = stage_col[1].astype(BF16)
    for k in range(4):
        at = (ROWS - 1) * (k // 2)
        corner_send[k] = jnp.broadcast_to(stage_col[k % 2, at : at + 1, :], (16, C)).astype(BF16)

    def halo(source, target, k, dx, dy):
        return pltpu.make_async_remote_copy(
            src_ref=source,
            dst_ref=target,
            send_sem=halo_send_sem.at[k],
            recv_sem=halo_sem.at[k],
            device_id=(gx + dx, gy + dy),
            device_id_type=MESH,
        )

    moves = [
        (bev.at[0], bottom, -1, 0),
        (bev.at[ROWS - 1], top, 1, 0),
        (col_send.at[0], col_recv.at[1], 0, -1),
        (col_send.at[1], col_recv.at[0], 0, 1),
        (corner_send.at[0], corner_recv.at[3], -1, -1),
        (corner_send.at[1], corner_recv.at[2], -1, 1),
        (corner_send.at[2], corner_recv.at[1], 1, -1),
        (corner_send.at[3], corner_recv.at[0], 1, 1),
    ]

    def inside(dx, dy):
        fine = jnp.logical_and(gx + dx >= 0, gx + dx < 16)
        return jnp.logical_and(fine, jnp.logical_and(gy + dy >= 0, gy + dy < 8))

    for k, (source, target, dx, dy) in enumerate(moves):
        @pl.when(inside(dx, dy))
        def _(source=source, target=target, dx=dx, dy=dy, k=k):
            halo(source, target, k, dx, dy).start()

    bias = bias_ref[...]

    def conv_row(above, here, below):
        window = jnp.concatenate([above, here, below], axis=1)
        return jnp.dot(window, wmat[...], preferred_element_type=F32)

    def finish(r, total):
        left = pltpu.roll(total[:, 0:C], 1, axis=0)
        right = pltpu.roll(total[:, 2 * C :], COLS - 1, axis=0)
        at = iota((COLS, C), 0)
        left = jnp.where(at == 0, edge[0, pl.ds(r, 1), :], left)
        right = jnp.where(at == COLS - 1, edge[1, pl.ds(r, 1), :], right)
        out = total[:, C : 2 * C] + left + right + bias
        conv_ref[r] = jnp.maximum(out, 0.0).astype(BF16)

    for k, (source, target, dx, dy) in enumerate(moves):
        @pl.when(inside(-dx, -dy))
        def _(source=source, target=target, dx=dx, dy=dy, k=k):
            halo(source, target, k, -dx, -dy).wait_recv()

    for side in range(2):
        ext[0:1, :] = corner_recv[side, 0:8, :].astype(F32)[0:1, :]
        ext[1:17, :] = col_recv[side].astype(F32)
        ext[17:18, :] = corner_recv[2 + side, 0:8, :].astype(F32)[0:1, :]
        window = jnp.concatenate([ext[0:16, :], ext[1:17, :], ext[2:18, :]], axis=1).astype(BF16)
        edge[side] = jnp.dot(
            window, wmat[:, 2 * side * C : (2 * side + 1) * C], preferred_element_type=F32
        )
    finish(0, conv_row(top[...], bev[0], bev[1]))

    def middle(r, carry):
        finish(r, conv_row(bev[r - 1], bev[r], bev[r + 1]))
        return carry

    lax.fori_loop(1, ROWS - 1, middle, 0)
    finish(ROWS - 1, conv_row(bev[ROWS - 2], bev[ROWS - 1], bottom[...]))

    for k, (source, target, dx, dy) in enumerate(moves):
        @pl.when(inside(dx, dy))
        def _(source=source, target=target, dx=dx, dy=dy, k=k):
            halo(source, target, k, dx, dy).wait_send()

    rest = pl.ds(1, DEV - 1)
    pltpu.make_async_copy(send.at[rest], send.at[rest], send_sem).wait()
    pltpu.make_async_copy(cells_in.at[rest], cells_in.at[rest], cell_send_sem).wait()


def shards(point_feats, point_tile, point_cell, point_count, conv_weight, conv_bias):
    vmem = pl.BlockSpec(memory_space=pltpu.VMEM)
    smem = pl.BlockSpec(memory_space=pltpu.SMEM)
    blocks = POINTS // BLOCK
    inv, cells = pl.pallas_call(
        index_kernel,
        name="index",
        out_shape=(
            jax.ShapeDtypeStruct((DEV, 128), jnp.int32),
            jax.ShapeDtypeStruct((DEV, 128), F32),
        ),
        in_specs=[vmem, vmem, smem],
        out_specs=(vmem, vmem),
        scratch_shapes=[pltpu.VMEM((DEV, 128), F32), pltpu.VMEM((DEV, 512), F32)],
    )(point_tile.reshape(blocks, BLOCK), point_cell.reshape(blocks, BLOCK), point_count)
    tile_map = jax.ShapeDtypeStruct((ROWS, COLS, C), BF16)
    dma = pltpu.SemaphoreType.DMA
    return pl.pallas_call(
        main_kernel,
        name="exchange",
        out_shape=(tile_map, tile_map),
        in_specs=[smem, vmem, vmem, vmem, vmem],
        out_specs=(vmem, vmem),
        scratch_shapes=[
            pltpu.VMEM((POINTS + 8, C), F32),
            pltpu.VMEM((CAP, C), F32),
            pltpu.VMEM((DEV, CAP, C), BF16),
            pltpu.VMEM((DEV, CAP, C), BF16),
            pltpu.VMEM((DEV, 1, 128), F32),
            pltpu.VMEM((ROWS // 2, COLS, 2 * C), F32),
            pltpu.VMEM((128, SPAN), BF16),
            pltpu.VMEM((COLS, SPAN), BF16),
            pltpu.VMEM((SPAN, C), BF16),
            pltpu.VMEM((GROUP, 128), F32),
            pltpu.VMEM((3 * C, 3 * C), BF16),
            pltpu.VMEM((ROWS, COLS, C), BF16),
            pltpu.VMEM((COLS, C), BF16),
            pltpu.VMEM((COLS, C), BF16),
            pltpu.VMEM((2, ROWS, C), BF16),
            pltpu.VMEM((2, ROWS, C), BF16),
            pltpu.VMEM((4, 16, C), BF16),
            pltpu.VMEM((4, 16, C), BF16),
            pltpu.VMEM((24, C), F32),
            pltpu.VMEM((2, ROWS, C), F32),
            pltpu.VMEM((2, ROWS, C), F32),
            dma,
            dma,
            dma((GROUPS,)),
            dma((GROUPS,)),
            dma((8,)),
            dma((8,)),
        ],
        compiler_params=pltpu.CompilerParams(
            collective_id=0, has_side_effects=True, vmem_limit_bytes=56 * 1024 * 1024
        ),
    )(inv, point_feats, cells.reshape(DEV, 1, 128), conv_weight, conv_bias.reshape(1, C))


def solution(mesh):
    in_specs = (
        P(("gx", "gy"), None),
        P(("gx", "gy"), None),
        P(("gx", "gy")),
        P(("gx", "gy")),
        P(),
        P(),
    )
    out_specs = (P("gx", "gy", None), P("gx", "gy", None))
    return jax.shard_map(shards, mesh=mesh, in_specs=in_specs, out_specs=out_specs, check_vma=False)
```

time: 405 us -> 87.7 us (0.22)
  the two profiles are of different devices: /device:TPU:7 before, /device:TPU:17 now
where the time goes in v1:
time: 87.7 us; the launch traced here: 87.3 us
  Pallas kernels  78.6 us (90%)
  local copies, waits for them, and re-layouts  5.87 us (7%)
  other arithmetic  1.48 us (2%)
  between operations  1.3 us (1%)
    pallas_call x1, Pallas kernels, shards(): pl.pallas_call(main_kernel, name='exchange', out_shape=(tile_map, tile_ma...  68.1 us
    pallas_call x1, Pallas kernels, shards(): pl.pallas_call(index_kernel, name='index', out_shape=(jax.ShapeDtypeStruc...  10.6 us
    unnamed x5, local copies, waits for them, and re-layouts  3.87 us

profile of v1, /device:TPU:17, one launch (start us, length us, event | category | flops | bytes accessed | tf_op | source)
XLA Modules:
  0.0 87.3 jit_solution(6612674138906074245)
XLA Ops:
  1.3 0.5 broadcast.3
  1.8 1.5 %reduce.3 = s32[8192]{0:T(1024)S(1)} reduce(s32[8192,1]{0,1:T(1,128)} %param.7, s32[]{:T(128)} %broadcast.3), dimensions={1}, to_apply=%param.7.reduce_sub_computation.3 | reduce | bytes 65540 | tf_op args[1]
  3.3 0.6 reshape.16.tile_ref
  3.9 1.4 %reshape.17.cell_ref = s32[16,512]{1,0:T(8,128)} reshape(s32[8192]{0:T(1024)} %param.8) | data formatting | bytes 65536 | tf_op jit(solution)/shard_map/reshape | solution.py:321
  5.3 10.6 %index.1 = (s32[128,128]{1,0:T(8,128)}, f32[128,128]{1,0:T(8,128)}) custom-call(s32[16,512]{1,0:T(8,128)} %reshape.16.tile_ref, s32[16,512]{1,0:T(8,128)} %reshape.17.cell_ref, s32[1]{0:T(128)S(6)} %copy.10.count_ref), custom_call_target="tpu_custom_call" | custom-call | tf_op jit(solution)/shard_map/index/pallas_call | solution.py:311
  15.8 68.1 %exchange.1 = (bf16[16,256,128]{2,1,0:T(8,128)(2,1)}, bf16[16,256,128]{2,1,0:T(8,128)(2,1)}) custom-call(s32[128,128]{1,0:T(8,128)} %get-tuple-element.4.inv_ref, bf16[8192,128]{1,0:T(8,128)(2,1)} %feats_ref.1, f32[128,1,128]{2,1,0:T(1,128)} %bitcast.3, bf16[3,3,128,128]{3,2,1,0:T(8,128)(2,1)} %w_ref.1, f32[1,128]{1,0:T(1,128)} %bitcast.4), custom_call_target="tpu_custom_call" | custom-call | tf_op jit(solution)/shard_map/exchange/pallas_call | solution.py:324
  83.9 0.0 copy-start
  83.9 2.4 %copy.11 = bf16[16,256,128]{2,1,0:T(8,128)(2,1)} copy(bf16[16,256,128]{2,1,0:T(8,128)(2,1)} %get-tuple-element.8) | data formatting | bytes 2097152
  86.3 0.0 copy-done
  86.3 1.0 %copy.12 = bf16[16,256,128]{2,1,0:T(8,128)(2,1)} copy(bf16[16,256,128]{2,1,0:T(8,128)(2,1)S(1)} %copy-done) | data formatting | bytes 2097152
Async XLA Ops:
  83.9 2.4 %copy-start = (bf16[16,256,128]{2,1,0:T(8,128)(2,1)S(1)}, bf16[16,256,128]{2,1,0:T(8,128)(2,1)}, u32[]{:S(2)}) copy-start(bf16[16,256,128]{2,1,0:T(8,128)(2,1)} %get-tuple-element.9) | copy-start | bytes 3145732

commit v2 on v1

v2 whole, which is shorter than its diff:
```python
import functools

import jax
import jax.numpy as jnp
from jax import lax
from jax.experimental import pallas as pl
from jax.experimental.pallas import tpu as pltpu
from jax.sharding import PartitionSpec as P

MESH = pl.DeviceIdType.MESH
F32 = jnp.float32
BF16 = jnp.bfloat16
C = 128
COLS = 256
ROWS = 16
POINTS = 8192
CAP = 80
DEV = 128
GROUP = 16
GROUPS = DEV // GROUP
SPAN = GROUP * CAP
STRIDE = 27
WIDTH = CAP + 2
BLOCK = 256
CHUNK = 2048


def iota(shape, dim):
    return lax.broadcasted_iota(jnp.int32, shape, dim)


def place():
    gx = lax.axis_index("gx")
    gy = lax.axis_index("gy")
    return lax.rem(gx, 4), lax.div(gx, 4), lax.div(gy, 2), lax.rem(gy, 2)


def partner(i):
    x, y, z, c = place()
    o = lax.rem(i * STRIDE, DEV)
    tc = lax.rem(c + lax.rem(o, 2), 2)
    tz = lax.rem(z + lax.rem(lax.div(o, 2), 4), 4)
    tx = lax.rem(x + lax.rem(lax.div(o, 8), 4), 4)
    ty = lax.rem(y + lax.div(o, 32), 4)
    return ty * 4 + tx, tz * 2 + tc


def main_kernel(
    tile_hbm, cell_hbm, count_ref, feats_hbm, w_hbm, bias_hbm, bev_hbm, conv_hbm,
    bev_ref, conv_ref, tile_ref, cell_ref, w_ref, bias_ref, feats, src, hits, values, table, offs, inv_vmem, inv, row_tab, col_tab,
    stage, send, recv, acc, expand, onehot, row_bc, xs, wmat, top, bottom,
    col_send, col_recv, corner_send, corner_recv, ext, edge, stage_col, edge_pre,
    load_sem, store_sem, inv_sem, send_sem, recv_sem, halo_send_sem, halo_sem,
):
    gx = lax.axis_index("gx")
    gy = lax.axis_index("gy")
    arrays = (
        (tile_hbm, tile_ref), (cell_hbm, cell_ref), (feats_hbm, feats), (w_hbm, w_ref),
        (bias_hbm, bias_ref),
    )
    loads = [pltpu.make_async_copy(a, b, load_sem.at[k]) for k, (a, b) in enumerate(arrays)]
    for load in loads:
        load.start()
    zero_row = jnp.zeros((COLS, C), BF16)
    top[...] = zero_row
    bottom[...] = zero_row
    col_recv[...] = jnp.zeros_like(col_recv)
    corner_recv[...] = jnp.zeros_like(corner_recv)

    barrier = pltpu.get_barrier_semaphore()

    def greet(i, carry):
        other = lax.rem(gx * 8 + gy + i, DEV)
        dest = (lax.div(other, 8), lax.rem(other, 8))
        pl.semaphore_signal(barrier, inc=1, device_id=dest, device_id_type=MESH)
        return carry

    lax.fori_loop(1, DEV, greet, 0)

    offs[...] = jnp.zeros_like(offs)
    table[...] = jnp.zeros_like(table)
    values[...] = jnp.zeros_like(values)
    loads[0].wait()
    loads[1].wait()
    upper = (iota((BLOCK, BLOCK), 0) <= iota((BLOCK, BLOCK), 1)).astype(F32).astype(BF16)
    count = count_ref[0]

    def index_chunk(n, carry):
        base = offs[...]
        for b in range(CHUNK // BLOCK):
            line = n * (CHUNK // 128) + 2 * b
            pair = [tile_ref[pl.ds(line + h, 1), :] for h in range(2)]
            tile = jnp.concatenate(pair, axis=1)
            pair = [cell_ref[pl.ds(line + h, 1), :] for h in range(2)]
            cell = jnp.concatenate(pair, axis=1)
            p = n * CHUNK + b * BLOCK + iota((1, BLOCK), 1)
            tile = jnp.where(p < count, tile, DEV)
            hit = iota((DEV, BLOCK), 0) == tile
            hit16 = hit.astype(F32).astype(BF16)
            span = slice(b * BLOCK, (b + 1) * BLOCK)
            hits[:, span] = hit16
            cum = jnp.dot(hit16, upper, preferred_element_type=F32)
            total = cum + jnp.concatenate([base, base], axis=1)
            rank = jnp.sum(jnp.where(hit, total, 0.0), axis=0, keepdims=True) - 1.0
            base = base + jnp.broadcast_to(cum[:, BLOCK - 1 :], (DEV, 128))
            slot = iota((CAP, BLOCK), 0).astype(F32) == rank
            coded = ((p >> 5) + 1, (p & 31) * 8 + (cell >> 9), (cell & 511) - 256)
            for v, value in enumerate(coded):
                part = jnp.where(slot, value.astype(F32), 0.0).astype(BF16)
                values[v * CAP : (v + 1) * CAP, span] = part
        offs[...] = base
        table[...] += lax.dot_general(
            hits[...], values[...], (((1,), (1,)), ((), ())), preferred_element_type=F32
        )
        return carry

    lax.fori_loop(0, POINTS // CHUNK, index_chunk, 0)
    found = table[...]
    first = found[:, 0:128].astype(jnp.int32)
    second = pltpu.roll(found, 256 - CAP, axis=1)[:, 0:128].astype(jnp.int32)
    third = pltpu.roll(found, 256 - 2 * CAP, axis=1)[:, 0:128].astype(jnp.int32)
    filled = first > 0
    inv_vmem[...] = jnp.where(filled, (first - 1) * 32 + (second >> 3), POINTS)
    inv_copy = pltpu.make_async_copy(inv_vmem, inv, inv_sem)
    inv_copy.start()
    cells = (second & 7) * 512 + third + 256
    row_tab[...] = jnp.where(filled, cells >> 8, -1).astype(F32)
    col_tab[...] = (cells & 255).astype(F32)

    loads[2].wait()

    def widen(b, carry):
        at = pl.multiple_of(b * 512, 512)
        src[pl.ds(at, 512), :] = feats[pl.ds(at, 512), :].astype(F32)
        return carry

    lax.fori_loop(0, POINTS // 512, widen, 0)
    src[pl.ds(POINTS, 8), :] = jnp.zeros((8, C), F32)
    stage[...] = jnp.zeros_like(stage)
    inv_copy.wait()
    pl.semaphore_wait(barrier, DEV - 1)

    def feat_copy(i):
        return pltpu.make_async_remote_copy(
            src_ref=send.at[i],
            dst_ref=recv.at[i],
            send_sem=send_sem,
            recv_sem=recv_sem.at[lax.div(i, GROUP)],
            device_id=partner(i),
            device_id_type=MESH,
        )

    def pack(tile):
        for k in range(CAP):
            at = jnp.minimum(jnp.maximum(inv[tile, k], 0), POINTS)
            stage[k : k + 1, :] = src[pl.ds(at, 1), :]
        stage[CAP : CAP + 1, :] = row_tab[pl.ds(tile, 1), :]
        stage[CAP + 1 : WIDTH, :] = col_tab[pl.ds(tile, 1), :]
        return stage[...].astype(BF16)[0:WIDTH]

    def pack_and_send(i, carry):
        dest = partner(i)
        send[i] = pack(dest[0] * 8 + dest[1])

        @pl.when(i > 1)
        def _():
            feat_copy(i - 1).start()

        return carry

    lax.fori_loop(1, DEV, pack_and_send, 0)
    feat_copy(DEV - 1).start()
    recv[0] = pack(gx * 8 + gy)

    loads[3].wait()
    loads[4].wait()
    for a in range(3):
        for b in range(3):
            wmat[a * C : (a + 1) * C, b * C : (b + 1) * C] = w_ref[a, b]
    acc[...] = jnp.zeros_like(acc)
    lane = iota((1, SPAN), 1).astype(F32)
    owner = jnp.floor((lane + 0.5) * (1.0 / CAP))
    within = lane - owner * CAP
    expand[...] = (iota((128, SPAN), 0).astype(F32) == within).astype(F32).astype(BF16)
    eye = iota((128, 128), 0) == iota((128, 128), 1)
    ones = jnp.ones((128, 128), BF16)
    mine = iota((GROUP, SPAN), 0).astype(F32) == owner

    def scatter(g):
        for j in range(GROUP):
            both = recv[g * GROUP + j, CAP:WIDTH, :].astype(F32)
            xs[j : j + 1, :] = both[0:1]
            xs[GROUP + j : GROUP + j + 1, :] = both[1:2]
        dense = jnp.dot(xs[...].astype(BF16), expand[...], preferred_element_type=F32)
        row_line = jnp.sum(jnp.where(mine, dense[0:GROUP], 0.0), axis=0, keepdims=True)
        col_line = jnp.sum(jnp.where(mine, dense[GROUP:], 0.0), axis=0, keepdims=True)
        onehot[...] = (iota((COLS, SPAN), 0).astype(F32) == col_line).astype(F32).astype(BF16)
        for q in range(SPAN // 128):
            span = slice(q * 128, (q + 1) * 128)
            diag = jnp.where(eye, row_line[:, span], 0.0).astype(BF16)
            row_bc[span, :] = jnp.dot(diag, ones, preferred_element_type=F32).astype(BF16)
        at = pl.ds(pl.multiple_of(g * GROUP, GROUP), GROUP)
        points = recv[at, 0:CAP, :].reshape(SPAN, C)
        rows = row_bc[...]
        none = jnp.zeros((), BF16)
        for pair in range(ROWS // 2):
            even = jnp.where(rows == jnp.asarray(2 * pair, BF16), points, none)
            odd = jnp.where(rows == jnp.asarray(2 * pair + 1, BF16), points, none)
            acc[pair] += jnp.dot(
                onehot[...], jnp.concatenate([even, odd], axis=1), preferred_element_type=F32
            )

    def landed(g, first):
        at = pl.ds(g * GROUP + first, GROUP - first)
        pltpu.make_async_copy(recv.at[at], recv.at[at], recv_sem.at[g]).wait()

    landed(0, 1)
    scatter(0)

    def absorb(g, carry):
        landed(g, 0)
        scatter(g)
        return carry

    lax.fori_loop(1, GROUPS, absorb, 0)

    def settle(r):
        line = acc[r // 2, :, (r % 2) * C : (r % 2 + 1) * C]
        bev_ref[r] = line.astype(BF16)
        stage_col[0, r : r + 1, :] = line[0:1, :]
        stage_col[1, r : r + 1, :] = line[COLS - 1 : COLS, :]

    def halo(source, target, k, dx, dy):
        return pltpu.make_async_remote_copy(
            src_ref=source,
            dst_ref=target,
            send_sem=halo_send_sem.at[k],
            recv_sem=halo_sem.at[k],
            device_id=(gx + dx, gy + dy),
            device_id_type=MESH,
        )

    moves = [
        (bev_ref.at[0], bottom, -1, 0),
        (bev_ref.at[ROWS - 1], top, 1, 0),
        (col_send.at[0], col_recv.at[1], 0, -1),
        (col_send.at[1], col_recv.at[0], 0, 1),
        (corner_send.at[0], corner_recv.at[3], -1, -1),
        (corner_send.at[1], corner_recv.at[2], -1, 1),
        (corner_send.at[2], corner_recv.at[1], 1, -1),
        (corner_send.at[3], corner_recv.at[0], 1, 1),
    ]

    def inside(dx, dy):
        fine = jnp.logical_and(gx + dx >= 0, gx + dx < 16)
        return jnp.logical_and(fine, jnp.logical_and(gy + dy >= 0, gy + dy < 8))

    def launch(which):
        for k in which:
            source, target, dx, dy = moves[k]

            @pl.when(inside(dx, dy))
            def _(source=source, target=target, dx=dx, dy=dy, k=k):
                halo(source, target, k, dx, dy).start()

    settle(0)
    settle(ROWS - 1)
    for k in range(4):
        at = (ROWS - 1) * (k // 2)
        corner_send[k] = jnp.broadcast_to(stage_col[k % 2, at : at + 1, :], (16, C)).astype(BF16)
    for r in range(1, ROWS - 1):
        settle(r)
        if r == 2:
            launch((0, 1))
        if r == 6:
            launch((4, 5, 6, 7))
    col_send[0] = stage_col[0].astype(BF16)
    col_send[1] = stage_col[1].astype(BF16)
    bias = bias_ref[...]
    at = iota((COLS, C), 0)

    def finish(r, total):
        left = jnp.where(at == 0, 0.0, pltpu.roll(total[:, 0:C], 1, axis=0))
        right = jnp.where(at == COLS - 1, 0.0, pltpu.roll(total[:, 2 * C :], COLS - 1, axis=0))
        out = total[:, C : 2 * C] + left + right + bias
        edge_pre[0, r] = out[0:16]
        edge_pre[1, r] = out[COLS - 16 :]
        conv_ref[r] = jnp.maximum(out, 0.0).astype(BF16)

    launch((2, 3))
    bev_store = pltpu.make_async_copy(bev_ref, bev_hbm, store_sem.at[0])
    bev_store.start()

    def middle(m, carry):
        r = 2 * m + 1
        rows = [bev_ref[r - 1 + q] for q in range(4)]
        window = jnp.concatenate(
            [jnp.concatenate(rows[q : q + 2], axis=0) for q in range(3)], axis=1
        )
        total = jnp.dot(window, wmat[...], preferred_element_type=F32)
        finish(r, total[0:COLS])
        finish(r + 1, total[COLS:])
        return carry

    lax.fori_loop(0, ROWS // 2 - 1, middle, 0)

    for k, (source, target, dx, dy) in enumerate(moves):
        @pl.when(inside(-dx, -dy))
        def _(source=source, target=target, dx=dx, dy=dy, k=k):
            halo(source, target, k, -dx, -dy).wait_recv()

    window = jnp.concatenate(
        [
            jnp.concatenate([top[...], bev_ref[ROWS - 2]], axis=0),
            jnp.concatenate([bev_ref[0], bev_ref[ROWS - 1]], axis=0),
            jnp.concatenate([bev_ref[1], bottom[...]], axis=0),
        ],
        axis=1,
    )
    total = jnp.dot(window, wmat[...], preferred_element_type=F32)
    finish(0, total[0:COLS])
    finish(ROWS - 1, total[COLS:])
    for side in range(2):
        ext[0:1, :] = corner_recv[side].astype(F32)[0:1, :]
        ext[1:17, :] = col_recv[side].astype(F32)
        ext[17:18, :] = corner_recv[2 + side].astype(F32)[0:1, :]
        window = jnp.concatenate([ext[0:16, :], ext[1:17, :], ext[2:18, :]], axis=1).astype(BF16)
        edge[side] = jnp.dot(
            window, wmat[:, 2 * side * C : (2 * side + 1) * C], preferred_element_type=F32
        )
    small = iota((16, C), 0)
    for r in range(ROWS):
        left = edge_pre[0, r] + jnp.where(small == 0, edge[0, r : r + 1, :], 0.0)
        conv_ref[r, 0:16, :] = jnp.maximum(left, 0.0).astype(BF16)
        right = edge_pre[1, r] + jnp.where(small == 15, edge[1, r : r + 1, :], 0.0)
        conv_ref[r, COLS - 16 :, :] = jnp.maximum(right, 0.0).astype(BF16)

    conv_store = pltpu.make_async_copy(conv_ref, conv_hbm, store_sem.at[1])
    conv_store.start()
    for k, (source, target, dx, dy) in enumerate(moves):
        @pl.when(inside(dx, dy))
        def _(source=source, target=target, dx=dx, dy=dy, k=k):
            halo(source, target, k, dx, dy).wait_send()

    rest = pl.ds(1, DEV - 1)
    pltpu.make_async_copy(send.at[rest], send.at[rest], send_sem).wait()
    bev_store.wait()
    conv_store.wait()


def shards(point_feats, point_tile, point_cell, point_count, conv_weight, conv_bias):
    smem = pl.BlockSpec(memory_space=pltpu.SMEM)
    hbm = pl.BlockSpec(memory_space=pltpu.HBM)
    tile_map = jax.ShapeDtypeStruct((ROWS, COLS, C), BF16)
    dma = pltpu.SemaphoreType.DMA
    return pl.pallas_call(
        main_kernel,
        name="exchange",
        out_shape=(tile_map, tile_map),
        in_specs=[hbm, hbm, smem, hbm, hbm, hbm],
        out_specs=(hbm, hbm),
        scratch_shapes=[
            pltpu.VMEM((ROWS, COLS, C), BF16),
            pltpu.VMEM((ROWS, COLS, C), BF16),
            pltpu.VMEM((POINTS // 128, 128), jnp.int32),
            pltpu.VMEM((POINTS // 128, 128), jnp.int32),
            pltpu.VMEM((3, 3, C, C), BF16),
            pltpu.VMEM((1, C), F32),
            pltpu.VMEM((POINTS, C), BF16),
            pltpu.VMEM((POINTS + 8, C), F32),
            pltpu.VMEM((DEV, CHUNK), BF16),
            pltpu.VMEM((256, CHUNK), BF16),
            pltpu.VMEM((DEV, 256), F32),
            pltpu.VMEM((DEV, 128), F32),
            pltpu.VMEM((DEV, 128), jnp.int32),
            pltpu.SMEM((DEV, 128), jnp.int32),
            pltpu.VMEM((DEV, 128), F32),
            pltpu.VMEM((DEV, 128), F32),
            pltpu.VMEM((96, C), F32),
            pltpu.VMEM((DEV, WIDTH, C), BF16),
            pltpu.VMEM((DEV, WIDTH, C), BF16),
            pltpu.VMEM((ROWS // 2, COLS, 2 * C), F32),
            pltpu.VMEM((128, SPAN), BF16),
            pltpu.VMEM((COLS, SPAN), BF16),
            pltpu.VMEM((SPAN, C), BF16),
            pltpu.VMEM((2 * GROUP, 128), F32),
            pltpu.VMEM((3 * C, 3 * C), BF16),
            pltpu.VMEM((COLS, C), BF16),
            pltpu.VMEM((COLS, C), BF16),
            pltpu.VMEM((2, ROWS, C), BF16),
            pltpu.VMEM((2, ROWS, C), BF16),
            pltpu.VMEM((4, 16, C), BF16),
            pltpu.VMEM((4, 16, C), BF16),
            pltpu.VMEM((24, C), F32),
            pltpu.VMEM((2, ROWS, C), F32),
            pltpu.VMEM((2, ROWS, C), F32),
            pltpu.VMEM((2, ROWS, 16, C), F32),
            dma((5,)),
            dma((2,)),
            dma,
            dma,
            dma((GROUPS,)),
            dma((8,)),
            dma((8,)),
        ],
        compiler_params=pltpu.CompilerParams(
            collective_id=0, has_side_effects=True, vmem_limit_bytes=63 * 1024 * 1024
        ),
    )(
        point_tile.reshape(POINTS // 128, 128),
        point_cell.reshape(POINTS // 128, 128),
        point_count,
        point_feats,
        conv_weight,
        conv_bias.reshape(1, C),
    )


def solution(mesh):
    in_specs = (
        P(("gx", "gy"), None),
        P(("gx", "gy"), None),
        P(("gx", "gy")),
        P(("gx", "gy")),
        P(),
        P(),
    )
    out_specs = (P("gx", "gy", None), P("gx", "gy", None))
    return jax.shard_map(shards, mesh=mesh, in_specs=in_specs, out_specs=out_specs, check_vma=False)
```

time: 87.7 us -> 65.9 us (0.75)
  the two profiles are of different devices: /device:TPU:17 before, /device:TPU:24 now
where the time goes in v2:
time: 65.9 us; the launch traced here: 65.8 us
  Pallas kernels  61.2 us (93%)
  local copies, waits for them, and re-layouts  3.36 us (5%)
  between operations  1.29 us (2%)
    pallas_call x1, Pallas kernels, shards(): pl.pallas_call(main_kernel, name='exchange', out_shape=(tile_map, tile_ma...  61.2 us
    unnamed x4, local copies, waits for them, and re-layouts  3.36 us

profile of v2, /device:TPU:24, one launch (start us, length us, event | category | flops | bytes accessed | tf_op | source)
XLA Modules:
  0.0 65.8 jit_solution(17235049849301351252)
XLA Ops:
  1.3 61.2 %exchange.1 = (bf16[16,256,128]{2,1,0:T(8,128)(2,1)}, bf16[16,256,128]{2,1,0:T(8,128)(2,1)}) custom-call(s32[64,128]{1,0:T(8,128)} %bitcast.3, s32[64,128]{1,0:T(8,128)} %bitcast.4, s32[1]{0:T(128)S(6)} %copy.10.count_ref, bf16[8192,128]{1,0:T(8,128)(2,1)} %feats_hbm.1, bf16[3,3,128,128]{3,2,1,0:T(8,128)(2,1)} %w_hbm.1, f32[1,128]{1,0:T(1,128)} %bitcast.5), custom_call_target="tpu_custom_call" | custom-call | tf_op jit(solution)/shard_map/exchange/pallas_call | solution.py:356
  62.4 0.0 copy-start
  62.4 2.4 %copy.11 = bf16[16,256,128]{2,1,0:T(8,128)(2,1)} copy(bf16[16,256,128]{2,1,0:T(8,128)(2,1)} %get-tuple-element.4) | data formatting | bytes 2097152
  64.8 0.0 copy-done
  64.8 1.0 %copy.12 = bf16[16,256,128]{2,1,0:T(8,128)(2,1)} copy(bf16[16,256,128]{2,1,0:T(8,128)(2,1)S(1)} %copy-done) | data formatting | bytes 2097152
Async XLA Ops:
  62.4 2.4 %copy-start = (bf16[16,256,128]{2,1,0:T(8,128)(2,1)S(1)}, bf16[16,256,128]{2,1,0:T(8,128)(2,1)}, u32[]{:S(2)}) copy-start(bf16[16,256,128]{2,1,0:T(8,128)(2,1)} %get-tuple-element.5) | copy-start | bytes 3145732

commit v3 on v2

--- a/solution.py
+++ b/solution.py
@@ -20,6 +20,7 @@
 GROUPS = DEV // GROUP
 SPAN = GROUP * CAP
 STRIDE = 27
+LAG = 4
 WIDTH = CAP + 2
 BLOCK = 256
 CHUNK = 2048
@@ -46,11 +47,11 @@
 
 
 def main_kernel(
-    tile_hbm, cell_hbm, count_ref, feats_hbm, w_hbm, bias_hbm, bev_hbm, conv_hbm,
-    bev_ref, conv_ref, tile_ref, cell_ref, w_ref, bias_ref, feats, src, hits, values, table, offs, inv_vmem, inv, row_tab, col_tab,
+    tile_hbm, cell_hbm, count_ref, feats_hbm, w_hbm, bias_hbm, bev_ref, conv_ref,
+    tile_ref, cell_ref, w_ref, bias_ref, feats, src, hits, values, table, offs, inv_vmem, inv, row_tab, col_tab,
     stage, send, recv, acc, expand, onehot, row_bc, xs, wmat, top, bottom,
     col_send, col_recv, corner_send, corner_recv, ext, edge, stage_col, edge_pre,
-    load_sem, store_sem, inv_sem, send_sem, recv_sem, halo_send_sem, halo_sem,
+    load_sem, inv_sem, send_sem, recv_sem, halo_send_sem, halo_sem,
 ):
     gx = lax.axis_index("gx")
     gy = lax.axis_index("gy")
@@ -85,8 +86,12 @@
     upper = (iota((BLOCK, BLOCK), 0) <= iota((BLOCK, BLOCK), 1)).astype(F32).astype(BF16)
     count = count_ref[0]
 
+    loads[2].wait()
+
     def index_chunk(n, carry):
         base = offs[...]
+        at = pl.multiple_of(n * CHUNK, CHUNK)
+        src[pl.ds(at, CHUNK), :] = feats[pl.ds(at, CHUNK), :].astype(F32)
         for b in range(CHUNK // BLOCK):
             line = n * (CHUNK // 128) + 2 * b
             pair = [tile_ref[pl.ds(line + h, 1), :] for h in range(2)]
@@ -127,14 +132,7 @@
     row_tab[...] = jnp.where(filled, cells >> 8, -1).astype(F32)
     col_tab[...] = (cells & 255).astype(F32)
 
-    loads[2].wait()
-
-    def widen(b, carry):
-        at = pl.multiple_of(b * 512, 512)
-        src[pl.ds(at, 512), :] = feats[pl.ds(at, 512), :].astype(F32)
-        return carry
-
-    lax.fori_loop(0, POINTS // 512, widen, 0)
+
     src[pl.ds(POINTS, 8), :] = jnp.zeros((8, C), F32)
     stage[...] = jnp.zeros_like(stage)
     inv_copy.wait()
@@ -157,20 +155,6 @@
         stage[CAP : CAP + 1, :] = row_tab[pl.ds(tile, 1), :]
         stage[CAP + 1 : WIDTH, :] = col_tab[pl.ds(tile, 1), :]
         return stage[...].astype(BF16)[0:WIDTH]
-
-    def pack_and_send(i, carry):
-        dest = partner(i)
-        send[i] = pack(dest[0] * 8 + dest[1])
-
-        @pl.when(i > 1)
-        def _():
-            feat_copy(i - 1).start()
-
-        return carry
-
-    lax.fori_loop(1, DEV, pack_and_send, 0)
-    feat_copy(DEV - 1).start()
-    recv[0] = pack(gx * 8 + gy)
 
     loads[3].wait()
     loads[4].wait()
@@ -214,15 +198,45 @@
         at = pl.ds(g * GROUP + first, GROUP - first)
         pltpu.make_async_copy(recv.at[at], recv.at[at], recv_sem.at[g]).wait()
 
-    landed(0, 1)
-    scatter(0)
+    recv[0] = pack(gx * 8 + gy)
 
     def absorb(g, carry):
-        landed(g, 0)
+        @pl.when(g == 0)
+        def _():
+            landed(0, 1)
+
+        @pl.when(g > 0)
+        def _():
+            landed(g, 0)
+
         scatter(g)
         return carry
 
-    lax.fori_loop(1, GROUPS, absorb, 0)
+    def batch(g, carry):
+        first = jnp.maximum(g * GROUP, 1)
+        end = (g + 1) * GROUP
+
+        def pack_and_send(i, carry):
+            dest = partner(i)
+            send[i] = pack(dest[0] * 8 + dest[1])
+
+            @pl.when(i > first)
+            def _():
+                feat_copy(i - 1).start()
+
+            return carry
+
+        lax.fori_loop(first, end, pack_and_send, 0)
+        feat_copy(end - 1).start()
+
+        @pl.when(g >= LAG)
+        def _():
+            absorb(g - LAG, 0)
+
+        return carry
+
+    lax.fori_loop(0, GROUPS, batch, 0)
+    lax.fori_loop(GROUPS - LAG, GROUPS, absorb, 0)
 
     def settle(r):
         line = acc[r // 2, :, (r % 2) * C : (r % 2 + 1) * C]
@@ -288,8 +302,6 @@
         conv_ref[r] = jnp.maximum(out, 0.0).astype(BF16)
 
     launch((2, 3))
-    bev_store = pltpu.make_async_copy(bev_ref, bev_hbm, store_sem.at[0])
-    bev_store.start()
 
     def middle(m, carry):
         r = 2 * m + 1
@@ -335,8 +347,6 @@
         right = edge_pre[1, r] + jnp.where(small == 15, edge[1, r : r + 1, :], 0.0)
         conv_ref[r, COLS - 16 :, :] = jnp.maximum(right, 0.0).astype(BF16)
 
-    conv_store = pltpu.make_async_copy(conv_ref, conv_hbm, store_sem.at[1])
-    conv_store.start()
     for k, (source, target, dx, dy) in enumerate(moves):
         @pl.when(inside(dx, dy))
         def _(source=source, target=target, dx=dx, dy=dy, k=k):
@@ -344,24 +354,21 @@
 
     rest = pl.ds(1, DEV - 1)
     pltpu.make_async_copy(send.at[rest], send.at[rest], send_sem).wait()
-    bev_store.wait()
-    conv_store.wait()
 
 
 def shards(point_feats, point_tile, point_cell, point_count, conv_weight, conv_bias):
     smem = pl.BlockSpec(memory_space=pltpu.SMEM)
+    vmem = pl.BlockSpec(memory_space=pltpu.VMEM)
     hbm = pl.BlockSpec(memory_space=pltpu.HBM)
-    tile_map = jax.ShapeDtypeStruct((ROWS, COLS, C), BF16)
+    tile_map = pltpu.VMEM((ROWS, COLS, C), BF16)
     dma = pltpu.SemaphoreType.DMA
     return pl.pallas_call(
         main_kernel,
         name="exchange",
         out_shape=(tile_map, tile_map),
         in_specs=[hbm, hbm, smem, hbm, hbm, hbm],
-        out_specs=(hbm, hbm),
+        out_specs=(vmem, vmem),
         scratch_shapes=[
-            pltpu.VMEM((ROWS, COLS, C), BF16),
-            pltpu.VMEM((ROWS, COLS, C), BF16),
             pltpu.VMEM((POINTS // 128, 128), jnp.int32),
             pltpu.VMEM((POINTS // 128, 128), jnp.int32),
             pltpu.VMEM((3, 3, C, C), BF16),
@@ -396,7 +403,6 @@
             pltpu.VMEM((2, ROWS, C), F32),
             pltpu.VMEM((2, ROWS, 16, C), F32),
             dma((5,)),
-            dma((2,)),
             dma,
             dma,
             dma((GROUPS,)),
@@ -404,7 +410,7 @@
             dma((8,)),
         ],
         compiler_params=pltpu.CompilerParams(
-            collective_id=0, has_side_effects=True, vmem_limit_bytes=63 * 1024 * 1024
+            collective_id=0, has_side_effects=True, vmem_limit_bytes=64929792
         ),
     )(
         point_tile.reshape(POINTS // 128, 128),

time: 65.9 us -> 62 us (0.941)
  the two profiles are of different devices: /device:TPU:24 before, /device:TPU:7 now
where the time goes in v3:
time: 62 us; the launch traced here: 61.3 us
  Pallas kernels  58 us (94%)
  local copies, waits for them, and re-layouts  1.94 us (3%)
  between operations  1.29 us (2%)
    pallas_call x1, Pallas kernels, shards(): pl.pallas_call(main_kernel, name='exchange', out_shape=(tile_map, tile_ma...  58 us
    unnamed x2, local copies, waits for them, and re-layouts  1.94 us

profile of v3, /device:TPU:7, one launch (start us, length us, event | category | flops | bytes accessed | tf_op | source)
XLA Modules:
  0.0 61.3 jit_solution(9849370213413742129)
XLA Ops:
  1.3 58.0 %exchange.1 = (bf16[16,256,128]{2,1,0:T(8,128)(2,1)S(1)}, bf16[16,256,128]{2,1,0:T(8,128)(2,1)S(1)}) custom-call(s32[64,128]{1,0:T(8,128)} %bitcast.3, s32[64,128]{1,0:T(8,128)} %bitcast.4, s32[1]{0:T(128)S(6)} %copy.12.count_ref, bf16[8192,128]{1,0:T(8,128)(2,1)} %feats_hbm.1, bf16[3,3,128,128]{3,2,1,0:T(8,128)(2,1)} %w_hbm.1, f32[1,128]{1,0:T(1,128)} %bitcast.5), custom_call_target="tpu_custom_call" | custom-call | tf_op jit(solution)/shard_map/exchange/pallas_call | solution.py:365
  59.3 1.0 %copy.10 = bf16[16,256,128]{2,1,0:T(8,128)(2,1)} copy(bf16[16,256,128]{2,1,0:T(8,128)(2,1)S(1)} %get-tuple-element.2) | data formatting | bytes 2097152
  60.3 1.0 %copy.11 = bf16[16,256,128]{2,1,0:T(8,128)(2,1)} copy(bf16[16,256,128]{2,1,0:T(8,128)(2,1)S(1)} %get-tuple-element.3) | data formatting | bytes 2097152

commit v4 on v3

--- a/solution.py
+++ b/solution.py
@@ -21,7 +21,6 @@
 SPAN = GROUP * CAP
 STRIDE = 27
 LAG = 4
-WIDTH = CAP + 2
 BLOCK = 256
 CHUNK = 2048
 
@@ -48,10 +47,10 @@
 
 def main_kernel(
     tile_hbm, cell_hbm, count_ref, feats_hbm, w_hbm, bias_hbm, bev_ref, conv_ref,
-    tile_ref, cell_ref, w_ref, bias_ref, feats, src, hits, values, table, offs, inv_vmem, inv, row_tab, col_tab,
+    tile_ref, cell_ref, w_ref, bias_ref, feats, src, hits, values, table, offs, inv_vmem, inv, cell_tab, cell_send, cells_in,
     stage, send, recv, acc, expand, onehot, row_bc, xs, wmat, top, bottom,
     col_send, col_recv, corner_send, corner_recv, ext, edge, stage_col, edge_pre,
-    load_sem, inv_sem, send_sem, recv_sem, halo_send_sem, halo_sem,
+    load_sem, inv_sem, send_sem, recv_sem, cell_send_sem, cell_sem, halo_send_sem, halo_sem,
 ):
     gx = lax.axis_index("gx")
     gy = lax.axis_index("gy")
@@ -129,53 +128,58 @@
     inv_copy = pltpu.make_async_copy(inv_vmem, inv, inv_sem)
     inv_copy.start()
     cells = (second & 7) * 512 + third + 256
-    row_tab[...] = jnp.where(filled, cells >> 8, -1).astype(F32)
-    col_tab[...] = (cells & 255).astype(F32)
+    cell_tab[...] = jnp.where(filled, cells, -1).astype(F32)
 
 
     src[pl.ds(POINTS, 8), :] = jnp.zeros((8, C), F32)
-    stage[...] = jnp.zeros_like(stage)
     inv_copy.wait()
     pl.semaphore_wait(barrier, DEV - 1)
 
-    def feat_copy(i):
+    def cell_copy(i, dest):
+        return pltpu.make_async_remote_copy(
+            src_ref=cell_send.at[i],
+            dst_ref=cells_in.at[i],
+            send_sem=cell_send_sem,
+            recv_sem=cell_sem.at[lax.div(i, GROUP)],
+            device_id=dest,
+            device_id_type=MESH,
+        )
+
+    def feat_copy(i, dest):
         return pltpu.make_async_remote_copy(
             src_ref=send.at[i],
             dst_ref=recv.at[i],
             send_sem=send_sem,
             recv_sem=recv_sem.at[lax.div(i, GROUP)],
-            device_id=partner(i),
+            device_id=dest,
             device_id_type=MESH,
         )
+
+    def ship(i):
+        dest = partner(i)
+        cell_copy(i, dest).start()
+        feat_copy(i, dest).start()
 
     def pack(tile):
         for k in range(CAP):
             at = jnp.minimum(jnp.maximum(inv[tile, k], 0), POINTS)
             stage[k : k + 1, :] = src[pl.ds(at, 1), :]
-        stage[CAP : CAP + 1, :] = row_tab[pl.ds(tile, 1), :]
-        stage[CAP + 1 : WIDTH, :] = col_tab[pl.ds(tile, 1), :]
-        return stage[...].astype(BF16)[0:WIDTH]
-
-    loads[3].wait()
-    loads[4].wait()
-    for a in range(3):
-        for b in range(3):
-            wmat[a * C : (a + 1) * C, b * C : (b + 1) * C] = w_ref[a, b]
-    acc[...] = jnp.zeros_like(acc)
+        return stage[...].astype(BF16)
+
     lane = iota((1, SPAN), 1).astype(F32)
     owner = jnp.floor((lane + 0.5) * (1.0 / CAP))
     within = lane - owner * CAP
-    expand[...] = (iota((128, SPAN), 0).astype(F32) == within).astype(F32).astype(BF16)
     eye = iota((128, 128), 0) == iota((128, 128), 1)
     ones = jnp.ones((128, 128), BF16)
     mine = iota((GROUP, SPAN), 0).astype(F32) == owner
 
     def scatter(g):
         for j in range(GROUP):
-            both = recv[g * GROUP + j, CAP:WIDTH, :].astype(F32)
-            xs[j : j + 1, :] = both[0:1]
-            xs[GROUP + j : GROUP + j + 1, :] = both[1:2]
-        dense = jnp.dot(xs[...].astype(BF16), expand[...], preferred_element_type=F32)
+            xs[j : j + 1, :] = cells_in[g * GROUP + j]
+        cell = xs[...]
+        row = jnp.floor(cell * (1.0 / COLS))
+        both = jnp.concatenate([row, cell - row * COLS], axis=0).astype(BF16)
+        dense = jnp.dot(both, expand[...], preferred_element_type=F32)
         row_line = jnp.sum(jnp.where(mine, dense[0:GROUP], 0.0), axis=0, keepdims=True)
         col_line = jnp.sum(jnp.where(mine, dense[GROUP:], 0.0), axis=0, keepdims=True)
         onehot[...] = (iota((COLS, SPAN), 0).astype(F32) == col_line).astype(F32).astype(BF16)
@@ -184,7 +188,7 @@
             diag = jnp.where(eye, row_line[:, span], 0.0).astype(BF16)
             row_bc[span, :] = jnp.dot(diag, ones, preferred_element_type=F32).astype(BF16)
         at = pl.ds(pl.multiple_of(g * GROUP, GROUP), GROUP)
-        points = recv[at, 0:CAP, :].reshape(SPAN, C)
+        points = recv[at].reshape(SPAN, C)
         rows = row_bc[...]
         none = jnp.zeros((), BF16)
         for pair in range(ROWS // 2):
@@ -196,9 +200,9 @@
 
     def landed(g, first):
         at = pl.ds(g * GROUP + first, GROUP - first)
+        pltpu.make_async_copy(cells_in.at[at], cells_in.at[at], cell_sem.at[g]).wait()
         pltpu.make_async_copy(recv.at[at], recv.at[at], recv_sem.at[g]).wait()
 
-    recv[0] = pack(gx * 8 + gy)
 
     def absorb(g, carry):
         @pl.when(g == 0)
@@ -212,22 +216,40 @@
         scatter(g)
         return carry
 
+    def setup():
+        loads[3].wait()
+        loads[4].wait()
+        for a in range(3):
+            for b in range(3):
+                wmat[a * C : (a + 1) * C, b * C : (b + 1) * C] = w_ref[a, b]
+        acc[...] = jnp.zeros_like(acc)
+        expand[...] = (iota((128, SPAN), 0).astype(F32) == within).astype(F32).astype(BF16)
+        own = gx * 8 + gy
+        recv[0] = pack(own)
+        cells_in[0] = cell_tab[pl.ds(own, 1), :]
+
     def batch(g, carry):
         first = jnp.maximum(g * GROUP, 1)
         end = (g + 1) * GROUP
 
         def pack_and_send(i, carry):
             dest = partner(i)
-            send[i] = pack(dest[0] * 8 + dest[1])
+            tile = dest[0] * 8 + dest[1]
+            send[i] = pack(tile)
+            cell_send[i] = cell_tab[pl.ds(tile, 1), :]
 
             @pl.when(i > first)
             def _():
-                feat_copy(i - 1).start()
+                ship(i - 1)
 
             return carry
 
         lax.fori_loop(first, end, pack_and_send, 0)
-        feat_copy(end - 1).start()
+        ship(end - 1)
+
+        @pl.when(g == 0)
+        def _():
+            setup()
 
         @pl.when(g >= LAG)
         def _():
@@ -354,6 +376,7 @@
 
     rest = pl.ds(1, DEV - 1)
     pltpu.make_async_copy(send.at[rest], send.at[rest], send_sem).wait()
+    pltpu.make_async_copy(cell_send.at[rest], cell_send.at[rest], cell_send_sem).wait()
 
 
 def shards(point_feats, point_tile, point_cell, point_count, conv_weight, conv_bias):
@@ -382,15 +405,16 @@
             pltpu.VMEM((DEV, 128), jnp.int32),
             pltpu.SMEM((DEV, 128), jnp.int32),
             pltpu.VMEM((DEV, 128), F32),
-            pltpu.VMEM((DEV, 128), F32),
-            pltpu.VMEM((96, C), F32),
-            pltpu.VMEM((DEV, WIDTH, C), BF16),
-            pltpu.VMEM((DEV, WIDTH, C), BF16),
+            pltpu.VMEM((DEV, 1, 128), F32),
+            pltpu.VMEM((DEV, 1, 128), F32),
+            pltpu.VMEM((CAP, C), F32),
+            pltpu.VMEM((DEV, CAP, C), BF16),
+            pltpu.VMEM((DEV, CAP, C), BF16),
             pltpu.VMEM((ROWS // 2, COLS, 2 * C), F32),
             pltpu.VMEM((128, SPAN), BF16),
             pltpu.VMEM((COLS, SPAN), BF16),
             pltpu.VMEM((SPAN, C), BF16),
-            pltpu.VMEM((2 * GROUP, 128), F32),
+            pltpu.VMEM((GROUP, 128), F32),
             pltpu.VMEM((3 * C, 3 * C), BF16),
             pltpu.VMEM((COLS, C), BF16),
             pltpu.VMEM((COLS, C), BF16),
@@ -404,6 +428,8 @@
             pltpu.VMEM((2, ROWS, 16, C), F32),
             dma((5,)),
             dma,
+            dma,
+            dma((GROUPS,)),
             dma,
             dma((GROUPS,)),
             dma((8,)),

time: 62 us -> 62.6 us (level)
  Pallas kernels: 58 us -> 58.7 us
    pallas_call x1, Pallas kernels: 58 us -> 58.7 us  [shards(): pl.pallas_call(main_kernel, name='exchange', out_shape=(tile_map, tile_ma...]
where the time goes in v4:
time: 62.6 us; the launch traced here: 61.9 us
  Pallas kernels  58.7 us (94%)
  local copies, waits for them, and re-layouts  1.94 us (3%)
  between operations  1.29 us (2%)
    pallas_call x1, Pallas kernels, shards(): pl.pallas_call(main_kernel, name='exchange', out_shape=(tile_map, tile_ma...  58.7 us
    unnamed x2, local copies, waits for them, and re-layouts  1.94 us

profile of v4, /device:TPU:7, one launch (start us, length us, event | category | flops | bytes accessed | tf_op | source)
XLA Modules:
  0.0 61.9 jit_solution(11538656448981205950)
XLA Ops:
  1.3 58.7 %exchange.1 = (bf16[16,256,128]{2,1,0:T(8,128)(2,1)S(1)}, bf16[16,256,128]{2,1,0:T(8,128)(2,1)S(1)}) custom-call(s32[64,128]{1,0:T(8,128)} %bitcast.3, s32[64,128]{1,0:T(8,128)} %bitcast.4, s32[1]{0:T(128)S(6)} %copy.12.count_ref, bf16[8192,128]{1,0:T(8,128)(2,1)} %feats_hbm.1, bf16[3,3,128,128]{3,2,1,0:T(8,128)(2,1)} %w_hbm.1, f32[1,128]{1,0:T(1,128)} %bitcast.5), custom_call_target="tpu_custom_call" | custom-call | tf_op jit(solution)/shard_map/exchange/pallas_call | solution.py:388
  60.0 1.0 %copy.10 = bf16[16,256,128]{2,1,0:T(8,128)(2,1)} copy(bf16[16,256,128]{2,1,0:T(8,128)(2,1)S(1)} %get-tuple-element.2) | data formatting | bytes 2097152
  61.0 1.0 %copy.11 = bf16[16,256,128]{2,1,0:T(8,128)(2,1)} copy(bf16[16,256,128]{2,1,0:T(8,128)(2,1)S(1)} %get-tuple-element.3) | data formatting | bytes 2097152
